TPU v7x, 32 devices: a whole 2x2x4 slice. The times are simulated.
32 devices in a mesh: dp: 8 (over z, core), tp: 4 (over y, x).
Axes of the slice: x: 2, y: 2, z: 4, core: 2. Of those that a mesh axis runs over, the one named last changes fastest.
Arguments:
- hidden_states: bfloat16 [2048, 3584], P('dp'), may hold values from -21 to 21
- resp_lengths: int32 [4], replicated, may hold values from 1 to 1280, 2048 in all
- w_query: bfloat16 [3584, 512], P('dp', 'tp'), may hold values from -0.25 to 0.25
- w_keyval: bfloat16 [3584, 1024], P('dp', 'tp'), may hold values from -0.09375 to 0.09375
- w_out: bfloat16 [512, 3584], P('tp', 'dp'), may hold values from -0.25 to 0.25
Outputs:
- attended: bfloat16 [2048, 3584], P('dp', 'tp')
Inputs may be any that keep to these rules, and one draw needn't show every extreme that they name: `resp_lengths`: the 4 lengths sum to 2048; the longest is exactly 1280.
All inputs are finite; a program needn't handle non-finite values.
Results may differ from a plain program's by a relative error of at most 0.015.
The roundings to bfloat16 on the way count: a program that leaves them out, or rounds other values in their place, can miss the bound.
Values may be sent and summed in bfloat16 or wider, within the bound.
A program may use at most 64 MiB of HBM per device.

v0:
```python
import jax
import jax.numpy as jnp
from jax import lax
from jax.sharding import PartitionSpec as P

HD = 128


def segment_of(position, resp_ends):
    return jnp.sum(
        (position[:, None] >= resp_ends[None, :]).astype(jnp.int32), axis=1, dtype=jnp.int32
    )


def body(hidden_states, resp_lengths, w_query, w_keyval, w_out):
    token_rows = hidden_states.shape[0]
    head_scale = HD ** (-0.5)
    pieces = (
        lax.all_gather(w_query, "dp", axis=0, tiled=True),
        lax.all_gather(w_keyval, "dp", axis=0, tiled=True),
    )
    query_sum = jnp.dot(hidden_states, pieces[0], preferred_element_type=jnp.float32)
    keyval_sum = jnp.dot(hidden_states, pieces[1], preferred_element_type=jnp.float32)
    query = (query_sum * head_scale).astype(jnp.bfloat16)
    keyval = lax.all_gather(keyval_sum.astype(jnp.bfloat16), "tp", axis=1, tiled=True)
    kv_count = keyval.shape[1] // (2 * HD)
    per_group = lax.axis_size("tp") // kv_count
    kv_head = lax.axis_index("tp") // per_group
    key_head = lax.dynamic_slice_in_dim(keyval, kv_head * HD, HD, 1)
    value_head = lax.dynamic_slice_in_dim(keyval, (kv_count + kv_head) * HD, HD, 1)
    head_pair = jnp.concatenate([key_head, value_head], axis=1)
    resp_ends = jnp.cumsum(resp_lengths, dtype=jnp.int32)
    own_begin = lax.axis_index("dp") * token_rows
    query_pos = own_begin + jnp.arange(token_rows, dtype=jnp.int32)
    query_seg = segment_of(query_pos, resp_ends)
    pieces = lax.all_gather(head_pair, "dp", axis=0, tiled=True)
    largest = jnp.full((token_rows,), -1e30, jnp.float32)
    height = pieces.shape[0]
    key_pos = jnp.arange(height, dtype=jnp.int32)
    key_seg = segment_of(key_pos, resp_ends)
    scores = jnp.dot(query, pieces[:, :HD].T, preferred_element_type=jnp.float32)
    allowed = (
        (query_seg[:, None] == key_seg[None, :])
        & (key_pos[None, :] <= query_pos[:, None])
        & (key_pos[None, :] >= 0)
    )
    newest = jnp.maximum(largest, jnp.max(jnp.where(allowed, scores, jnp.float32(-1e30)), axis=1))
    expw = jnp.where(allowed, jnp.exp(scores - newest[:, None]), jnp.float32(0.0))
    denom = jnp.sum(expw, axis=1)
    numer = jnp.dot(expw.astype(jnp.bfloat16), pieces[:, HD:], preferred_element_type=jnp.float32)
    heads_out = (numer / denom[:, None]).astype(jnp.bfloat16)
    terms = jnp.dot(
        heads_out,
        lax.all_gather(w_out, "dp", axis=1, tiled=True),
        preferred_element_type=jnp.float32,
    )
    summed = lax.psum_scatter(terms.astype(jnp.bfloat16), "tp", scatter_dimension=1, tiled=True)
    return summed


def solution(mesh):
    return jax.shard_map(
        body,
        mesh=mesh,
        in_specs=(P("dp", None), P(), P("dp", "tp"), P("dp", "tp"), P("tp", "dp")),
        out_specs=P("dp", "tp"),
        check_vma=False,
    )
```

profile of v0, /device:TPU:25, one launch (start us, length us, event | category | flops | bytes accessed | tf_op | source)
XLA Modules:
  0.0 144.8 jit_solution(7602217867818827257)
XLA Ops:
  6.5 0.0 copy-start
  6.5 0.0 all-gather.3.cloned.1.call-start
  6.5 0.7 all-gather.3.cloned.1.call-update
  7.3 0.0 all-gather.5.cloned.1.call-start
  7.3 0.0 copy-start.3
  7.3 0.0 copy-start.1
  7.3 28.5 %all-gather.3.cloned.1.call-done = bf16[3584,256]{1,0:T(8,128)(2,1)} async-done(((bf16[448,256]{1,0:T(8,128)(2,1)}), bf16[3584,256]{1,0:T(8,128)(2,1)}) %all-gather.3.cloned.1.call-update) | async-done | bytes 1835024 | tf_op jit(solution)/shard_map/all_gather | solution.py:20
  35.9 0.0 copy-done
  35.9 2.1 %convolution_convert_fusion.1 = bf16[256,256]{1,0:T(8,128)(2,1)S(1)} fusion(bf16[256,3584]{1,0:T(8,128)(2,1)S(1)} %copy-done, bf16[3584,256]{1,0:T(8,128)(2,1)} %all-gather.3.cloned.1.call-done), kind=kOutput, calls=%fused_computation.7 | convolution fusion | flops 469827584 | bytes 3801088 | tf_op jit(solution)/shard_map/dot_general | solution.py:23
  38.0 0.0 copy-start.2
  38.0 12.9 %all_gather.17 = bf16[256,1024]{1,0:T(8,128)(2,1)S(1)} all-gather(bf16[256,256]{1,0:T(8,128)(2,1)S(1)} %convolution_convert_fusion.1), channel_id=1, replica_groups=mesh['dp'=8,'tp'=4] {'tp'}, dimensions={1}, use_global_device_ids=true | all-gather | bytes 655360 | tf_op jit(solution)/shard_map/all_gather | solution.py:25
  51.0 0.7 pad_maximum_fusion
  51.7 0.0 all-gather.5.cloned.1.call-update
  51.7 0.0 reduce-scatter.4.cloned.1.call-start
  51.8 0.0 copy-done.3
  51.8 0.2 reduce-window.8
  51.9 0.1 convert_reduce_fusion
  52.0 0.1 convert_reduce_fusion.1
  52.1 0.0 copy-done.1
  52.1 21.1 %all_gather.15 = bf16[3584,128]{1,0:T(8,128)(2,1)} all-gather(bf16[448,128]{1,0:T(8,128)(2,1)S(1)} %copy-done.1), channel_id=1, replica_groups=mesh['dp'=8,'tp'=4] {'dp'}, dimensions={0}, use_global_device_ids=true | all-gather | bytes 1032192 | tf_op jit(solution)/shard_map/all_gather | solution.py:19
  73.2 0.0 copy-done.2
  73.2 16.3 %all_gather.19 = bf16[128,3584]{0,1:T(8,128)(2,1)S(1)} all-gather(bf16[128,448]{0,1:T(8,128)(2,1)S(1)} %copy-done.2), channel_id=1, replica_groups=mesh['dp'=8,'tp'=4] {'dp'}, dimensions={1}, use_global_device_ids=true | all-gather | bytes 1032192 | tf_op jit(solution)/shard_map/all_gather | solution.py:54
  89.5 0.0 all-gather.5.cloned.1.call-done
  89.5 3.8 %select_reduce_fusion = (f32[256]{0:T(256)S(1)}, f32[256,2048]{1,0:T(8,128)}) fusion(s32[256]{0:T(256)S(1)} %iota_add_fusion, s32[2048]{0:T(1024)S(1)} %convert_reduce_fusion, s32[256]{0:T(256)S(1)} %convert_reduce_fusion.1, bf16[2048,256]{1,0:T(8,128)(2,1)} %all-gather.5.cloned.1.call-done, bf16[256,3584]{1,0:T(8,128)(2,1)S(1)} %copy-done, ...), kind=kOutput, calls=%fused_computation.2 | convolution fusion | flops 371785472 | bytes 5385216 | tf_op jit(solution)/shard_map/dot_general | solution.py:41
  93.2 2.3 %fusion.1 = f32[256]{0:T(256)S(1)} fusion(f32[256,2048]{1,0:T(8,128)} %get-tuple-element.8, f32[256]{0:T(256)S(1)} %broadcast_maximum_fusion, s32[256]{0:T(256)S(1)} %iota_add_fusion, s32[2048]{0:T(1024)S(1)} %convert_reduce_fusion, s32[256]{0:T(256)S(1)} %convert_reduce_fusion.1), kind=kLoop, calls=%fused_computation.5 | loop fusion | flops 3145472 | bytes 2109440 | tf_op jit(solution)/shard_map/reduce_sum | solution.py:49
  95.6 4.2 %convolution_convert_fusion = bf16[256,3584]{1,0:T(8,128)(2,1)} fusion(bf16[128,3584]{0,1:T(8,128)(2,1)S(1)} %all_gather.19, f32[256,2048]{1,0:T(8,128)} %get-tuple-element.8, f32[256]{0:T(256)S(1)} %broadcast_maximum_fusion, s32[256]{0:T(256)S(1)} %iota_add_fusion, s32[2048]{0:T(1024)S(1)} %convert_reduce_fusion, s32[256]{0:T(256)S(1)} %convert_reduce_fusion.1, ...), kind=kOutput, calls=%fused_computation | convolution fusion | flops 373227520 | bytes 5386240 | tf_op jit(solution)/shard_map/dot_general | solution.py:52
  99.8 3.8 %copy.6 = bf16[256,3584]{0,1:T(8,128)(2,1)} copy(bf16[256,3584]{1,0:T(8,128)(2,1)} %convolution_convert_fusion) | data formatting | bytes 3670016
  103.6 0.0 reduce-scatter.4.cloned.1.call-update
  103.6 32.7 %reduce-scatter.4.cloned.1.call-done = bf16[896,256]{1,0:T(8,128)(2,1)} async-done(((bf16[3584,256]{1,0:T(8,128)(2,1)}), bf16[896,256]{1,0:T(8,128)(2,1)}) %reduce-scatter.4.cloned.1.call-update) | async-done | bytes 458768
  136.3 2.0 %copy.7 = bf16[256,896]{1,0:T(8,128)(2,1)} copy(bf16[256,896]{0,1:T(8,128)(2,1)} %bitcast.10) | data formatting | bytes 917504
  (3 shorter events, 0.0 us)
Async XLA Ops:
  6.5 29.3 %copy-start = (bf16[256,3584]{1,0:T(8,128)(2,1)S(1)}, bf16[256,3584]{1,0:T(8,128)(2,1)}, u32[]{:S(2)}) copy-start(bf16[256,3584]{1,0:T(8,128)(2,1)} %param.5) | copy-start | bytes 5505028
  6.5 29.3 %all-gather.3.cloned.1.call-start = ((), (), s32[]{:S(2)}) async-start(), calls=%async_computation.1 | async-start | bytes 2064384 | tf_op jit(solution)/shard_map/all_gather | solution.py:20
  7.3 82.2 %all-gather.5.cloned.1.call-start = ((), (), s32[]{:S(2)}) async-start(), calls=%async_computation.2 | async-start | bytes 1179648 | tf_op jit(solution)/shard_map/all_gather | solution.py:36
  7.3 44.4 %copy-start.3 = (s32[4]{0:T(128)S(1)}, s32[4]{0:T(128)}, u32[]{:S(2)}) copy-start(s32[4]{0:T(128)} %param.6) | copy-start | bytes 52
  7.3 44.8 %copy-start.1 = (bf16[448,128]{1,0:T(8,128)(2,1)S(1)}, bf16[448,128]{1,0:T(8,128)(2,1)}, u32[]{:S(2)}) copy-start(bf16[448,128]{1,0:T(8,128)(2,1)} %param.7) | copy-start | bytes 344068
  38.0 35.2 %copy-start.2 = (bf16[128,448]{0,1:T(8,128)(2,1)S(1)}, bf16[128,448]{0,1:T(8,128)(2,1)}, u32[]{:S(2)}) copy-start(bf16[128,448]{0,1:T(8,128)(2,1)} %param.9) | copy-start | bytes 344068
  51.7 84.6 %reduce-scatter.4.cloned.1.call-start = ((), (), s32[]{:S(2)}) async-start(), calls=%async_computation.3 | async-start | bytes 2293760
Sparse Core Ops, SparseCore 0:
  9.0 26.8 all-gather.2
  51.8 25.3 all-gather.4
  103.8 32.4 reduce-scatter.3
where the time goes:
time: 147 us; the launch traced here: 145 us
  waiting for transfers between devices  61.9 us (42%)
  blocking collectives  50.3 us (34%)
  between operations  13.2 us (9%)
  matrix products  10.1 us (7%)
  local copies, waits for them, and re-layouts  5.87 us (4%)
  other arithmetic  3.38 us (2%)
    unnamed x4, waiting for transfers between devices  33.4 us
    all_gather x1, waiting for transfers between devices, body(): lax.all_gather(w_keyval, 'dp', axis=0, tiled=True)  28.5 us
    all_gather x1, blocking collectives, body(): lax.all_gather(w_query, 'dp', axis=0, tiled=True)  21.1 us
    all_gather x1, blocking collectives, body(): lax.all_gather(w_out, 'dp', axis=1, tiled=True)  16.3 us
    all_gather x1, blocking collectives, body(): lax.all_gather(keyval_sum.astype(jnp.bfloat16), 'tp', axis=1, tiled=True)  12.9 us
    unnamed x10, local copies, waits for them, and re-layouts  5.84 us
    dot_general x1, matrix products, body(): jnp.dot(heads_out, lax.all_gather(w_out, 'dp', axis=1, tiled=True), prefe...  4.21 us
    dot_general x1, matrix products, body(): jnp.dot(query, pieces[:, :HD].T, preferred_element_type=jnp.float32)  3.76 us
  transfers between devices with their start and end apart: 3, of which 2 were waited for; matrix products, arithmetic and copies ran while one was open for 0% of the time, Pallas kernels for 0%

commit v1 on v0

--- a/solution.py
+++ b/solution.py
@@ -1,6 +1,10 @@
+import functools
+
 import jax
 import jax.numpy as jnp
 from jax import lax
+from jax.experimental import pallas as pl
+from jax.experimental.pallas import tpu as pltpu
 from jax.sharding import PartitionSpec as P
 
 HD = 128
@@ -58,9 +62,420 @@
     return summed
 
 
+MESH = pl.DeviceIdType.MESH
+KVA, KVB, WQ, WO, KD = range(5)
+
+
+def fused_kernel(
+    nz, nt, lens_ref, hid_hbm, wq_hbm, wkv_hbm, wo_hbm, out_ref,
+    hid, wq, wkv, woc, wof, kvloc, kvb, kvacc, qacc, qbuf, scores, mref, lref, oacc, hloc, hcat,
+    loc_sem, ss, rs, prs, kv_ss, kv_rs, wi_ss, wi_rs, wp_ss, wp_rs, h_ss, h_rs,
+):
+    dp = lax.axis_index("dp")
+    t = lax.axis_index("tp")
+    z, c = dp // 2, dp % 2
+    rows = hid.shape[0]
+    shard = wq_hbm.shape[0]
+    half = shard // 2
+    nout = wo_hbm.shape[1]
+
+    loads = [
+        pltpu.make_async_copy(wkv_hbm, wkv.at[pl.ds(dp * shard, shard)], loc_sem.at[0]),
+        pltpu.make_async_copy(wq_hbm, wq.at[pl.ds(dp * shard, shard)], loc_sem.at[1]),
+        pltpu.make_async_copy(hid_hbm, hid, loc_sem.at[2]),
+        pltpu.make_async_copy(wo_hbm, woc.at[z], loc_sem.at[3]),
+    ]
+    for load in loads:
+        load.start()
+
+    barrier = pltpu.get_barrier_semaphore()
+    partner = {"dp": dp + 1 - 2 * c, "tp": t}
+    up, down = {"dp": dp + 2, "tp": t}, {"dp": dp - 2, "tp": t}
+    has_up, has_down = z < nz - 1, z > 0
+    pl.semaphore_signal(barrier, 1, device_id=partner, device_id_type=MESH)
+
+    @pl.when(has_up)
+    def _():
+        pl.semaphore_signal(barrier, 1, device_id=up, device_id_type=MESH)
+
+    @pl.when(has_down)
+    def _():
+        pl.semaphore_signal(barrier, 1, device_id=down, device_id_type=MESH)
+
+    for k in range(1, nt):
+        pl.semaphore_signal(
+            barrier, 1, device_id={"dp": dp, "tp": (t + k) % nt}, device_id_type=MESH
+        )
+    pl.semaphore_wait(barrier, nt + has_up.astype(jnp.int32) + has_down.astype(jnp.int32))
+
+    def slot(item, zz, cc):
+        if item == KVA:
+            return wkv.at[pl.ds((2 * zz + cc) * shard, half)]
+        if item == KVB:
+            return wkv.at[pl.ds((2 * zz + cc) * shard + half, half)]
+        if item == WQ:
+            return wq.at[pl.ds((2 * zz + cc) * shard, shard)]
+        if item == WO:
+            return woc.at[zz]
+        return kvb.at[2 * zz + cc]
+
+    def chain(item, zz, way):
+        ref = slot(item, zz, c)
+        if way == 2:
+            recv, to = prs.at[item, zz], partner
+        else:
+            recv, to = rs.at[item, zz], (up if way == 0 else down)
+        return pltpu.make_async_remote_copy(
+            ref, ref, ss.at[item, zz, way], recv, device_id=to, device_id_type=MESH
+        )
+
+    def from_chain(item, zz):
+        ref = slot(item, zz, c)
+        pltpu.make_async_remote_copy(
+            ref, ref, ss.at[item, zz, 0], rs.at[item, zz], device_id=partner, device_id_type=MESH
+        ).wait_recv()
+
+    def from_partner(item, zz):
+        ref = slot(item, zz, 1 - c)
+        pltpu.make_async_remote_copy(
+            ref, ref, ss.at[item, zz, 2], prs.at[item, zz], device_id=partner, device_id_type=MESH
+        ).wait_recv()
+
+    def own_moves(item, act):
+        @pl.when(has_up)
+        def _():
+            act(chain(item, z, 0))
+
+        if item != KD:
+            @pl.when(has_down)
+            def _():
+                act(chain(item, z, 1))
+
+        if item == KD:
+            @pl.when(c == 0)
+            def _():
+                act(chain(item, z, 2))
+        elif item != WO:
+            act(chain(item, z, 2))
+
+    def passed_moves(item, k, below, act):
+        zz = z - k if below else z + k
+        if below:
+            @pl.when(has_up)
+            def _():
+                act(chain(item, zz, 0))
+        else:
+            @pl.when(has_down)
+            def _():
+                act(chain(item, zz, 1))
+        if item != WO:
+            act(chain(item, zz, 2))
+
+    def start(copy):
+        copy.start()
+
+    def wait_send(copy):
+        copy.wait_send()
+
+    def in_plane(zz):
+        return pltpu.make_async_remote_copy(
+            woc.at[zz], wof.at[c, pl.ds(t * HD, HD)], wi_ss.at[zz], wi_rs.at[t],
+            device_id={"dp": dp, "tp": zz}, device_id_type=MESH,
+        )
+
+    def take_wo(zz):
+        @pl.when(zz != t)
+        def _():
+            in_plane(zz).start()
+
+        @pl.when(zz == t)
+        def _():
+            wof[c, pl.ds(pl.multiple_of(t * HD, HD), HD), :] = woc[zz]
+            own_wo(zz).start()
+
+    def own_wo(zz):
+        return pltpu.make_async_remote_copy(
+            woc.at[zz], wof.at[c, pl.ds(t * HD, HD)], wp_ss.at[t], wp_rs.at[t],
+            device_id=partner, device_id_type=MESH,
+        )
+
+    def pass_on(item, k):
+        @pl.when(z - k >= 0)
+        def _():
+            from_chain(item, z - k)
+            passed_moves(item, k, True, start)
+            if item == WO:
+                take_wo(z - k)
+
+        if item != KD:
+            @pl.when(z + k < nz)
+            def _():
+                from_chain(item, z + k)
+                passed_moves(item, k, False, start)
+                if item == WO:
+                    take_wo(z + k)
+
+    def each_side(k, fn):
+        @pl.when(z - k >= 0)
+        def _():
+            fn(z - k)
+
+        @pl.when(z + k < nz)
+        def _():
+            fn(z + k)
+
+    def hidden_part(zz):
+        return hid[:, pl.ds(pl.multiple_of(zz * 2 * shard, 128), 2 * shard)]
+
+    def add_kv(zz):
+        from_partner(KVA, zz)
+        from_partner(KVB, zz)
+        weights = wkv[pl.ds(pl.multiple_of(zz * 2 * shard, 16), 2 * shard), :]
+        kvacc[...] += jnp.dot(hidden_part(zz), weights, preferred_element_type=jnp.float32)
+
+    def add_q(zz):
+        from_partner(WQ, zz)
+        weights = wq[pl.ds(pl.multiple_of(zz * 2 * shard, 16), 2 * shard), :]
+        qacc[...] += jnp.dot(hidden_part(zz), weights, preferred_element_type=jnp.float32)
+
+    loads[0].wait()
+    own_moves(KVA, start)
+    own_moves(KVB, start)
+    loads[1].wait()
+    loads[2].wait()
+    loads[3].wait()
+    kvacc[...] = jnp.zeros_like(kvacc)
+    qacc[...] = jnp.zeros_like(qacc)
+    add_kv(z)
+    for k in range(1, nz):
+        pass_on(KVA, k)
+        pass_on(KVB, k)
+        if k == nz - 1:
+            own_moves(WQ, start)
+        each_side(k, add_kv)
+
+    role = t // (nt // 2)
+    for h in range(2):
+        kvloc[h] = kvacc[:, h * HD:(h + 1) * HD].astype(jnp.bfloat16)
+
+    def kv_send(h):
+        return pltpu.make_async_remote_copy(
+            kvloc.at[h], kvb.at[dp, role], kv_ss.at[h], kv_rs.at[role],
+            device_id={"dp": dp, "tp": 2 * (t % (nt // 2)) + h}, device_id_type=MESH,
+        )
+
+    for h in range(2):
+        to = 2 * (t % (nt // 2)) + h
+
+        @pl.when(to != t)
+        def _():
+            kv_send(h).start()
+
+        @pl.when(to == t)
+        def _():
+            kvb[dp, role] = kvloc[h]
+
+    add_q(z)
+    for k in range(1, nz):
+        pass_on(WQ, k)
+        if k == 1:
+            for r in range(2):
+                @pl.when(t // 2 + r * (nt // 2) != t)
+                def _():
+                    pltpu.make_async_remote_copy(
+                        kvloc.at[r], kvb.at[dp, r], kv_ss.at[r], kv_rs.at[r],
+                        device_id=partner, device_id_type=MESH,
+                    ).wait_recv()
+
+            own_moves(KD, start)
+
+            @pl.when(c == 0)
+            def _():
+                kvb[dp + 1] = jnp.zeros(kvb.shape[1:], kvb.dtype)
+
+        if k == nz - 1:
+            own_moves(WO, start)
+            take_wo(z)
+        each_side(k, add_q)
+    qbuf[...] = (qacc[...] * (HD ** -0.5)).astype(jnp.bfloat16)
+
+    qpos = dp * rows + lax.broadcasted_iota(jnp.int32, (rows, 1), 0)
+    first = jnp.zeros((rows, 1), jnp.int32)
+    end = jnp.int32(0)
+    for r in range(lens_ref.shape[0]):
+        end = end + lens_ref[r]
+        first = jnp.where(qpos >= end, end, first)
+
+    def pair(zz, which):
+        return jnp.concatenate([kvb[2 * zz, which], kvb[2 * zz + 1, which]], axis=0)
+
+    def score(zz):
+        s = lax.dot_general(
+            qbuf[...], pair(zz, 0), (((1,), (1,)), ((), ())), preferred_element_type=jnp.float32
+        )
+        kpos = zz * 2 * rows + lax.broadcasted_iota(jnp.int32, s.shape, 1)
+        s = jnp.where((kpos >= first) & (kpos <= qpos), s, jnp.float32(-1e30))
+        scores[zz] = s
+        mref[...] = jnp.maximum(mref[...], jnp.max(s, axis=1, keepdims=True))
+
+    mref[...] = jnp.full_like(mref, -1e30)
+    for k in range(nz):
+        if k == 0:
+            @pl.when(c == 1)
+            def _():
+                from_partner(KD, z)
+            score(z)
+        else:
+            pass_on(KD, k)
+            pass_on(WO, k)
+
+            @pl.when(z - k >= 0)
+            def _():
+                from_partner(KD, z - k)
+                score(z - k)
+
+    lref[...] = jnp.zeros_like(lref)
+    oacc[...] = jnp.zeros_like(oacc)
+
+    def weigh(zz):
+        p = jnp.exp(scores[zz] - mref[...])
+        lref[...] += jnp.sum(p, axis=1, keepdims=True)
+        oacc[...] += jnp.dot(p.astype(jnp.bfloat16), pair(zz, 1), preferred_element_type=jnp.float32)
+
+    for k in range(nz):
+        @pl.when(z - k >= 0)
+        def _():
+            weigh(z - k)
+
+    heads = (oacc[...] / lref[...]).astype(jnp.bfloat16)
+    hloc[...] = heads
+    hcat[t] = heads
+
+    def head_copy(k):
+        return pltpu.make_async_remote_copy(
+            hloc, hcat.at[t], h_ss.at[k], h_rs.at[t],
+            device_id={"dp": dp, "tp": (t + k) % nt}, device_id_type=MESH,
+        )
+
+    for k in range(1, nt):
+        head_copy(k).start()
+
+    def wo_block(g, cc):
+        return wof.at[cc, pl.ds(g * HD, HD)]
+
+    def wo_partner(g):
+        return pltpu.make_async_remote_copy(
+            wo_block(g, c), wo_block(g, c), wp_ss.at[g], wp_rs.at[g],
+            device_id=partner, device_id_type=MESH,
+        )
+
+    for k in range(1, nt):
+        g = (t + k) % nt
+        pltpu.make_async_remote_copy(
+            woc.at[0], wo_block(g, c), wi_ss.at[0], wi_rs.at[g],
+            device_id=partner, device_id_type=MESH,
+        ).wait_recv()
+        wo_partner(g).start()
+    for g in range(nt):
+        pltpu.make_async_remote_copy(
+            woc.at[0], wo_block(g, 1 - c), wp_ss.at[g], wp_rs.at[g],
+            device_id=partner, device_id_type=MESH,
+        ).wait_recv()
+    for k in range(1, nt):
+        g = (t + k) % nt
+        pltpu.make_async_remote_copy(
+            hloc, hcat.at[g], h_ss.at[k], h_rs.at[g], device_id=partner, device_id_type=MESH
+        ).wait_recv()
+    every = jnp.concatenate([hcat[g] for g in range(nt)], axis=1)
+    for cc in range(2):
+        out_ref[:, cc * nout:(cc + 1) * nout] = jnp.dot(
+            every, wof[cc], preferred_element_type=jnp.float32
+        ).astype(out_ref.dtype)
+
+    for item in (KVA, KVB, WQ, WO, KD):
+        own_moves(item, wait_send)
+        for k in range(1, nz):
+            @pl.when(z - k >= 0)
+            def _():
+                passed_moves(item, k, True, wait_send)
+
+            if item != KD:
+                @pl.when(z + k < nz)
+                def _():
+                    passed_moves(item, k, False, wait_send)
+    for h in range(2):
+        @pl.when(2 * (t % (nt // 2)) + h != t)
+        def _():
+            kv_send(h).wait_send()
+    for k in range(1, nt):
+        head_copy(k).wait_send()
+        wo_partner((t + k) % nt).wait_send()
+        in_plane((t + k) % nt).wait_send()
+    own_wo(t).wait_send()
+
+
+def fused_body(nz, nt, hidden_states, resp_lengths, w_query, w_keyval, w_out):
+    rows, depth = hidden_states.shape
+    nout = w_out.shape[1]
+    bf16, f32 = jnp.bfloat16, jnp.float32
+    dma = pltpu.SemaphoreType.DMA
+    hbm = pl.BlockSpec(memory_space=pltpu.HBM)
+    return pl.pallas_call(
+        functools.partial(fused_kernel, nz, nt),
+        out_shape=jax.ShapeDtypeStruct((rows, 2 * nout), bf16),
+        in_specs=[pl.BlockSpec(memory_space=pltpu.SMEM), hbm, hbm, hbm, hbm],
+        out_specs=pl.BlockSpec(memory_space=pltpu.VMEM),
+        scratch_shapes=[
+            pltpu.VMEM((rows, depth), bf16),
+            pltpu.VMEM((depth, w_query.shape[1]), bf16),
+            pltpu.VMEM((depth, w_keyval.shape[1]), bf16),
+            pltpu.VMEM((nz, HD, nout), bf16),
+            pltpu.VMEM((2, nt * HD, nout), bf16),
+            pltpu.VMEM((2, rows, HD), bf16),
+            pltpu.VMEM((2 * nz, 2, rows, HD), bf16),
+            pltpu.VMEM((rows, 2 * HD), f32),
+            pltpu.VMEM((rows, HD), f32),
+            pltpu.VMEM((rows, HD), bf16),
+            pltpu.VMEM((nz, rows, 2 * rows), f32),
+            pltpu.VMEM((rows, 1), f32),
+            pltpu.VMEM((rows, 1), f32),
+            pltpu.VMEM((rows, HD), f32),
+            pltpu.VMEM((rows, HD), bf16),
+            pltpu.VMEM((nt, rows, HD), bf16),
+            dma((4,)),
+            dma((5, nz, 3)),
+            dma((5, nz)),
+            dma((5, nz)),
+            dma((2,)),
+            dma((2,)),
+            dma((nz,)),
+            dma((nt,)),
+            dma((nt,)),
+            dma((nt,)),
+            dma((nt,)),
+            dma((nt,)),
+        ],
+        compiler_params=pltpu.CompilerParams(
+            collective_id=0, has_side_effects=True, vmem_limit_bytes=50 * 1024 * 1024
+        ),
+    )(resp_lengths, hidden_states, w_query, w_keyval, w_out)
+
+
+def per_device(mesh, hidden_states, resp_lengths, w_query, w_keyval, w_out):
+    nt = mesh.shape["tp"]
+    nz = mesh.shape["dp"] // 2
+    args = (hidden_states, resp_lengths, w_query, w_keyval, w_out)
+    fits = (
+        mesh.shape["dp"] == 2 * nz and nz == nt and nt % 2 == 0
+        and w_query.shape[1] == HD and w_keyval.shape[1] == 2 * HD
+        and w_out.shape[0] == HD and w_query.shape[0] % 64 == 0
+    )
+    return fused_body(nz, nt, *args) if fits else body(*args)
+
+
 def solution(mesh):
     return jax.shard_map(
-        body,
+        functools.partial(per_device, mesh),
         mesh=mesh,
         in_specs=(P("dp", None), P(), P("dp", "tp"), P("dp", "tp"), P("tp", "dp")),
         out_specs=P("dp", "tp"),

time: 147 us -> 64.4 us (0.44); the launches traced: 145 us -> 64.2 us
  waiting for transfers between devices: 61.9 us -> 0 us
  Pallas kernels: 0 us -> 58.4 us
  blocking collectives: 50.3 us -> 0 us
  between operations: 13.2 us -> 0.03 us
  matrix products: 10.1 us -> 0 us
  other arithmetic: 3.38 us -> 0 us
    pallas_call x0 -> x1, Pallas kernels: none -> 58.4 us  [fused_body(): pl.pallas_call(functools.partial(fused_kernel, nz, nt), out_shape=jax.Sha...]
    all_gather x3 -> x0, blocking collectives: 50.3 us -> none  [the longest x1 21.1 us: body(): lax.all_gather(w_query, 'dp', axis=0, tiled=True)]
    unnamed x4 -> x0, waiting for transfers between devices: 33.4 us -> none
    all_gather x2 -> x0, waiting for transfers between devices: 28.5 us -> none  [the longest x1 28.5 us: body(): lax.all_gather(w_keyval, 'dp', axis=0, tiled=True)]
    dot_general x3 -> x0, matrix products: 10.1 us -> none  [the longest x1 4.21 us: body(): jnp.dot(heads_out, lax.all_gather(w_out, 'dp', axis=1, tiled=True), prefe...]
    reduce_sum x3 -> x0, other arithmetic: 2.52 us -> none  [the longest x1 2.34 us: body(): denom = jnp.sum(expw, axis=1)]
  transfers between devices with their start and end apart: 3 -> 0, of which waited for: 2 -> 0; matrix products, arithmetic and copies ran while one was open for 0% -> 0% of each run, Pallas kernels for 0% -> 0%
where the time goes in v1:
time: 64.4 us; the launch traced here: 64.2 us
  Pallas kernels  58.4 us (91%)
  local copies, waits for them, and re-layouts  5.75 us (9%)
    pallas_call x1, Pallas kernels, fused_body(): pl.pallas_call(functools.partial(fused_kernel, nz, nt), out_shape=jax.Sha...  58.4 us
    unnamed x10, local copies, waits for them, and re-layouts  5.75 us

profile of v1, /device:TPU:25, one launch (start us, length us, event | category | flops | bytes accessed | tf_op | source)
XLA Modules:
  0.0 64.2 jit_solution(1551256412095991789)
XLA Ops:
  0.0 1.0 %copy.6.wo_hbm = bf16[128,448]{1,0:T(8,128)(2,1)S(1)} copy(bf16[128,448]{0,1:T(8,128)(2,1)} %param.9) | data formatting | bytes 229376 | tf_op args[4]
  1.0 0.0 copy-start
  1.0 1.5 %copy-done = bf16[256,3584]{1,0:T(8,128)(2,1)S(1)} copy-done((bf16[256,3584]{1,0:T(8,128)(2,1)S(1)}, bf16[256,3584]{1,0:T(8,128)(2,1)}, u32[]{:S(2)}) %copy-start) | copy-done | bytes 1835032
  2.5 0.0 copy-start.1
  2.5 0.9 %copy-done.1 = bf16[448,256]{1,0:T(8,128)(2,1)S(1)} copy-done((bf16[448,256]{1,0:T(8,128)(2,1)S(1)}, bf16[448,256]{1,0:T(8,128)(2,1)}, u32[]{:S(2)}) %copy-start.1) | copy-done | bytes 229400
  3.4 0.0 copy-start.2
  3.5 0.9 %copy-done.2 = bf16[448,128]{1,0:T(8,128)(2,1)S(1)} copy-done((bf16[448,128]{1,0:T(8,128)(2,1)S(1)}, bf16[448,128]{1,0:T(8,128)(2,1)}, u32[]{:S(2)}) %copy-start.2) | copy-done | bytes 114712
  4.3 0.0 copy-start.3
  4.3 0.7 %copy-done.3 = s32[4]{0:T(128)S(1)} copy-done((s32[4]{0:T(128)S(1)}, s32[4]{0:T(128)}, u32[]{:S(2)}) %copy-start.3) | copy-done | bytes 40
  5.0 58.4 %shard_map.55 = bf16[256,896]{1,0:T(8,128)(2,1)S(1)} custom-call(s32[4]{0:T(128)S(1)} %copy-done.3, bf16[256,3584]{1,0:T(8,128)(2,1)S(1)} %copy-done, bf16[448,128]{1,0:T(8,128)(2,1)S(1)} %copy-done.2, bf16[448,256]{1,0:T(8,128)(2,1)S(1)} %copy-done.1, bf16[128,448]{1,0:T(8,128)(2,1)S(1)} %copy.6.wo_hbm), custom_call_target="tpu_custom_call" | custom-call | tf_op jit(solution)/shard_map/pallas_call | solution.py:423
  63.5 0.8 %copy.8 = bf16[256,896]{1,0:T(8,128)(2,1)} copy(bf16[256,896]{1,0:T(8,128)(2,1)S(1)} %shard_map.55) | data formatting | bytes 917504
Async XLA Ops:
  1.0 1.5 %copy-start = (bf16[256,3584]{1,0:T(8,128)(2,1)S(1)}, bf16[256,3584]{1,0:T(8,128)(2,1)}, u32[]{:S(2)}) copy-start(bf16[256,3584]{1,0:T(8,128)(2,1)} %hid_hbm.1) | copy-start | bytes 5505028
  2.5 0.9 %copy-start.1 = (bf16[448,256]{1,0:T(8,128)(2,1)S(1)}, bf16[448,256]{1,0:T(8,128)(2,1)}, u32[]{:S(2)}) copy-start(bf16[448,256]{1,0:T(8,128)(2,1)} %wkv_hbm.1) | copy-start | bytes 688132
  3.4 0.9 %copy-start.2 = (bf16[448,128]{1,0:T(8,128)(2,1)S(1)}, bf16[448,128]{1,0:T(8,128)(2,1)}, u32[]{:S(2)}) copy-start(bf16[448,128]{1,0:T(8,128)(2,1)} %wq_hbm.1) | copy-start | bytes 344068
  4.3 0.7 %copy-start.3 = (s32[4]{0:T(128)S(1)}, s32[4]{0:T(128)}, u32[]{:S(2)}) copy-start(s32[4]{0:T(128)} %lens_ref.1) | copy-start | bytes 52

commit v2 on v1

--- a/solution.py
+++ b/solution.py
@@ -63,7 +63,7 @@
 
 
 MESH = pl.DeviceIdType.MESH
-KVA, KVB, WQ, WO, KD = range(5)
+KVA, KVB, WQ, WO, KEY, VAL = range(6)
 
 
 def fused_kernel(
@@ -77,7 +77,7 @@
     rows = hid.shape[0]
     shard = wq_hbm.shape[0]
     half = shard // 2
-    nout = wo_hbm.shape[1]
+    nout = wo_hbm.shape[0]
 
     loads = [
         pltpu.make_async_copy(wkv_hbm, wkv.at[pl.ds(dp * shard, shard)], loc_sem.at[0]),
@@ -117,7 +117,7 @@
             return wq.at[pl.ds((2 * zz + cc) * shard, shard)]
         if item == WO:
             return woc.at[zz]
-        return kvb.at[2 * zz + cc]
+        return kvb.at[2 * zz + cc, 0 if item == KEY else 1]
 
     def chain(item, zz, way):
         ref = slot(item, zz, c)
@@ -146,12 +146,12 @@
         def _():
             act(chain(item, z, 0))
 
-        if item != KD:
+        if item not in (KEY, VAL):
             @pl.when(has_down)
             def _():
                 act(chain(item, z, 1))
 
-        if item == KD:
+        if item in (KEY, VAL):
             @pl.when(c == 0)
             def _():
                 act(chain(item, z, 2))
@@ -177,9 +177,12 @@
     def wait_send(copy):
         copy.wait_send()
 
+    def wo_block(g, cc):
+        return wof.at[pl.ds(pl.multiple_of(cc * nout, 16), nout), pl.ds(pl.multiple_of(g * HD, HD), HD)]
+
     def in_plane(zz):
         return pltpu.make_async_remote_copy(
-            woc.at[zz], wof.at[c, pl.ds(t * HD, HD)], wi_ss.at[zz], wi_rs.at[t],
+            woc.at[zz], wo_block(t, c), wi_ss.at[zz], wi_rs.at[t],
             device_id={"dp": dp, "tp": zz}, device_id_type=MESH,
         )
 
@@ -190,12 +193,12 @@
 
         @pl.when(zz == t)
         def _():
-            wof[c, pl.ds(pl.multiple_of(t * HD, HD), HD), :] = woc[zz]
+            wo_block(t, c)[...] = woc[zz]
             own_wo(zz).start()
 
     def own_wo(zz):
         return pltpu.make_async_remote_copy(
-            woc.at[zz], wof.at[c, pl.ds(t * HD, HD)], wp_ss.at[t], wp_rs.at[t],
+            woc.at[zz], wo_block(t, c), wp_ss.at[t], wp_rs.at[t],
             device_id=partner, device_id_type=MESH,
         )
 
@@ -207,7 +210,7 @@
             if item == WO:
                 take_wo(z - k)
 
-        if item != KD:
+        if item not in (KEY, VAL):
             @pl.when(z + k < nz)
             def _():
                 from_chain(item, z + k)
@@ -241,9 +244,7 @@
     loads[0].wait()
     own_moves(KVA, start)
     own_moves(KVB, start)
-    loads[1].wait()
     loads[2].wait()
-    loads[3].wait()
     kvacc[...] = jnp.zeros_like(kvacc)
     qacc[...] = jnp.zeros_like(qacc)
     add_kv(z)
@@ -251,7 +252,11 @@
         pass_on(KVA, k)
         pass_on(KVB, k)
         if k == nz - 1:
+            loads[1].wait()
             own_moves(WQ, start)
+            loads[3].wait()
+            own_moves(WO, start)
+            take_wo(z)
         each_side(k, add_kv)
 
     role = t // (nt // 2)
@@ -287,15 +292,14 @@
                         device_id=partner, device_id_type=MESH,
                     ).wait_recv()
 
-            own_moves(KD, start)
+            own_moves(KEY, start)
+            own_moves(VAL, start)
 
             @pl.when(c == 0)
             def _():
                 kvb[dp + 1] = jnp.zeros(kvb.shape[1:], kvb.dtype)
 
-        if k == nz - 1:
-            own_moves(WO, start)
-            take_wo(z)
+        pass_on(WO, k)
         each_side(k, add_q)
     qbuf[...] = (qacc[...] * (HD ** -0.5)).astype(jnp.bfloat16)
 
@@ -323,21 +327,27 @@
         if k == 0:
             @pl.when(c == 1)
             def _():
-                from_partner(KD, z)
+                from_partner(KEY, z)
             score(z)
         else:
-            pass_on(KD, k)
-            pass_on(WO, k)
+            pass_on(KEY, k)
+            pass_on(VAL, k)
 
             @pl.when(z - k >= 0)
             def _():
-                from_partner(KD, z - k)
+                from_partner(KEY, z - k)
                 score(z - k)
 
     lref[...] = jnp.zeros_like(lref)
     oacc[...] = jnp.zeros_like(oacc)
 
-    def weigh(zz):
+    def weigh(zz, k):
+        if k > 0:
+            from_partner(VAL, zz)
+        else:
+            @pl.when(c == 1)
+            def _():
+                from_partner(VAL, zz)
         p = jnp.exp(scores[zz] - mref[...])
         lref[...] += jnp.sum(p, axis=1, keepdims=True)
         oacc[...] += jnp.dot(p.astype(jnp.bfloat16), pair(zz, 1), preferred_element_type=jnp.float32)
@@ -345,23 +355,23 @@
     for k in range(nz):
         @pl.when(z - k >= 0)
         def _():
-            weigh(z - k)
+            weigh(z - k, k)
+
+    def head_cols(g):
+        return hcat.at[:, pl.ds(pl.multiple_of(g * HD, HD), HD)]
 
     heads = (oacc[...] / lref[...]).astype(jnp.bfloat16)
     hloc[...] = heads
-    hcat[t] = heads
+    head_cols(t)[...] = heads
 
     def head_copy(k):
         return pltpu.make_async_remote_copy(
-            hloc, hcat.at[t], h_ss.at[k], h_rs.at[t],
+            hloc, head_cols(t), h_ss.at[k], h_rs.at[t],
             device_id={"dp": dp, "tp": (t + k) % nt}, device_id_type=MESH,
         )
 
     for k in range(1, nt):
         head_copy(k).start()
-
-    def wo_block(g, cc):
-        return wof.at[cc, pl.ds(g * HD, HD)]
 
     def wo_partner(g):
         return pltpu.make_async_remote_copy(
@@ -384,22 +394,20 @@
     for k in range(1, nt):
         g = (t + k) % nt
         pltpu.make_async_remote_copy(
-            hloc, hcat.at[g], h_ss.at[k], h_rs.at[g], device_id=partner, device_id_type=MESH
+            hloc, head_cols(g), h_ss.at[k], h_rs.at[g], device_id=partner, device_id_type=MESH
         ).wait_recv()
-    every = jnp.concatenate([hcat[g] for g in range(nt)], axis=1)
-    for cc in range(2):
-        out_ref[:, cc * nout:(cc + 1) * nout] = jnp.dot(
-            every, wof[cc], preferred_element_type=jnp.float32
-        ).astype(out_ref.dtype)
-
-    for item in (KVA, KVB, WQ, WO, KD):
+    out_ref[...] = lax.dot_general(
+        hcat[...], wof[...], (((1,), (1,)), ((), ())), preferred_element_type=jnp.float32
+    ).astype(out_ref.dtype)
+
+    for item in (KVA, KVB, WQ, WO, KEY, VAL):
         own_moves(item, wait_send)
         for k in range(1, nz):
             @pl.when(z - k >= 0)
             def _():
                 passed_moves(item, k, True, wait_send)
 
-            if item != KD:
+            if item not in (KEY, VAL):
                 @pl.when(z + k < nz)
                 def _():
                     passed_moves(item, k, False, wait_send)
@@ -429,8 +437,8 @@
             pltpu.VMEM((rows, depth), bf16),
             pltpu.VMEM((depth, w_query.shape[1]), bf16),
             pltpu.VMEM((depth, w_keyval.shape[1]), bf16),
-            pltpu.VMEM((nz, HD, nout), bf16),
-            pltpu.VMEM((2, nt * HD, nout), bf16),
+            pltpu.VMEM((nz, nout, HD), bf16),
+            pltpu.VMEM((2 * nout, nt * HD), bf16),
             pltpu.VMEM((2, rows, HD), bf16),
             pltpu.VMEM((2 * nz, 2, rows, HD), bf16),
             pltpu.VMEM((rows, 2 * HD), f32),
@@ -441,11 +449,11 @@
             pltpu.VMEM((rows, 1), f32),
             pltpu.VMEM((rows, HD), f32),
             pltpu.VMEM((rows, HD), bf16),
-            pltpu.VMEM((nt, rows, HD), bf16),
+            pltpu.VMEM((rows, nt * HD), bf16),
             dma((4,)),
-            dma((5, nz, 3)),
-            dma((5, nz)),
-            dma((5, nz)),
+            dma((6, nz, 3)),
+            dma((6, nz)),
+            dma((6, nz)),
             dma((2,)),
             dma((2,)),
             dma((nz,)),
@@ -456,9 +464,9 @@
             dma((nt,)),
         ],
         compiler_params=pltpu.CompilerParams(
-            collective_id=0, has_side_effects=True, vmem_limit_bytes=50 * 1024 * 1024
+            collective_id=0, has_side_effects=True, vmem_limit_bytes=67_000_000
         ),
-    )(resp_lengths, hidden_states, w_query, w_keyval, w_out)
+    )(resp_lengths, hidden_states, w_query, w_keyval, w_out.T)
 
 
 def per_device(mesh, hidden_states, resp_lengths, w_query, w_keyval, w_out):

time: 64.4 us -> 53.2 us (0.83)
  Pallas kernels: 58.4 us -> 51.2 us
  local copies, waits for them, and re-layouts: 5.75 us -> 1.82 us
    pallas_call x1, Pallas kernels: 58.4 us -> 51.2 us  [fused_body(): pl.pallas_call(functools.partial(fused_kernel, nz, nt), out_shape=jax.Sha...]
    unnamed x10 -> x1, local copies, waits for them, and re-layouts: 5.75 us -> 1.82 us
where the time goes in v2:
time: 53.2 us; the launch traced here: 53.1 us
  Pallas kernels  51.2 us (96%)
  local copies, waits for them, and re-layouts  1.82 us (3%)
    pallas_call x1, Pallas kernels, fused_body(): pl.pallas_call(functools.partial(fused_kernel, nz, nt), out_shape=jax.Sha...  51.2 us
    unnamed x1, local copies, waits for them, and re-layouts  1.82 us

profile of v2, /device:TPU:25, one launch (start us, length us, event | category | flops | bytes accessed | tf_op | source)
XLA Modules:
  0.0 53.1 jit_solution(2214421337764863038)
XLA Ops:
  0.0 51.2 %shard_map.55 = bf16[256,896]{1,0:T(8,128)(2,1)} custom-call(s32[4]{0:T(128)} %lens_ref.1, bf16[256,3584]{1,0:T(8,128)(2,1)} %hid_hbm.1, bf16[448,128]{1,0:T(8,128)(2,1)} %wq_hbm.1, bf16[448,256]{1,0:T(8,128)(2,1)} %wkv_hbm.1, bf16[448,128]{1,0:T(8,128)(2,1)} %bitcast.1), custom_call_target="tpu_custom_call" | custom-call | tf_op jit(solution)/shard_map/pallas_call | solution.py:431
  51.2 1.8 %copy.7 = bf16[256,896]{1,0:T(8,128)(2,1)} copy(bf16[256,896]{1,0:T(8,128)(2,1)} %shard_map.55) | data formatting | bytes 917504
